TPU v7x, 512 devices: a whole 4x8x8 slice. The times are simulated.
512 devices in a mesh: gx: 8 (over y), gy: 64 (over x, z, core).
Axes of the slice: x: 4, y: 8, z: 8, core: 2. Of those that a mesh axis runs over, the one named last changes fastest.
Arguments:
- basis_mats: float32 [12, 275, 275], replicated, may hold values from -8 to 8.5, as said below
- coeffs: float32 [8192, 12], P(('gx', 'gy')), may hold values from 0.5 to 2
- element_loads: float32 [8192, 275], P(('gx', 'gy')), may hold values from -18 to 18
- elem_faces: int32 [8192, 6], P(('gx', 'gy')), may hold values from 0 to 71, as said below
- orient_codes: int32 [8192, 6], P(('gx', 'gy')), may hold values from 0 to 7
- shared_owned: int32 [512, 2, 4], P(('gx', 'gy')), may hold values from 0 to 63, as said below
- shared_remote: int32 [512, 2, 4], P(('gx', 'gy')), may hold values from 0 to 7, as said below
- lower_peers: int32 [512, 2], P(('gx', 'gy')), may hold values from 0 to 511, as said below
- upper_peers: int32 [512, 2], P(('gx', 'gy')), may hold values from 0 to 511, as said below
Outputs:
- trace: float32 [25, 32768], P(None, ('gx', 'gy'))
- residual: float32 [25, 32768], P(None, ('gx', 'gy'))
Inputs may be any that keep to these rules, and one draw needn't show every extreme that they name: `basis_mats`: each matrix is symmetric with every eigenvalue at least 0.5. `elem_faces`: an entry below 64 is a face slot that the element's device owns; an entry 64 + r is that device's remote slot r. Every owned slot of a device is named by one or two of its element faces, every remote slot by exactly one. `shared_owned`: row (d, i) lists 4 distinct owned slots of device d, in message order, that device lower_peers[d, i] uses; the two rows of a device are disjoint. `shared_remote`: row (d, i) lists remote slots of device d in message order: its k-th entry is the face that device upper_peers[d, i] lists k-th in its row i of shared_owned. The two rows of a device together hold each of its 8 remote slots once. upper_peers[lower_peers[d, i], i] = d for every device d and i; the two entries of a row differ. Peers are arbitrary device numbers. lower_peers[upper_peers[d, i], i] = d for every device d and i; the two entries of a row differ; each column is a permutation of the devices. Peers are arbitrary device numbers.
All inputs are finite; a program needn't handle non-finite values.
Results may differ from a plain program's by a relative error of at most 0.0003.
Values sent between devices are 32-bit elements; how exact they have to be, the bound alone decides.
No kernel may reach another device: no remote copies, remote signals or barrier semaphores. Data moves between devices by JAX's collectives and lax.ppermute only.
A program may use at most 128 MiB of HBM per device.

v0:
```python
import math
import jax
import jax.numpy as jnp
import numpy as np
from jax import lax
from jax.sharding import PartitionSpec as P

SIDE = 5
FACE_DOFS = 25
CELL_DOFS = 125
TRACE_DOFS = 150
ITERS = 4
FACE_DEV = 64
SHARED = 4
REMOTE = 8
full_precision = lax.Precision.HIGHEST


def orient_table():
    edge_nodes = SIDE
    codes_table = np.zeros((8, edge_nodes * edge_nodes), np.int32)
    for code_index in range(8):
        for first_axis in range(edge_nodes):
            for second_axis in range(edge_nodes):
                if code_index & 1:
                    first_new, second_new = (second_axis, first_axis)
                else:
                    first_new, second_new = (first_axis, second_axis)
                if code_index & 2:
                    first_new = edge_nodes - 1 - first_new
                if code_index & 4:
                    second_new = edge_nodes - 1 - second_new
                codes_table[code_index, first_axis * edge_nodes + second_axis] = (
                    first_new * edge_nodes + second_new
                )
    return codes_table


def permute_mats():
    codes_table = orient_table()
    matrices = np.zeros((8, FACE_DOFS, FACE_DOFS), np.float32)
    for code_index in range(8):
        for position in range(FACE_DOFS):
            matrices[code_index, position, codes_table[code_index, position]] = 1.0
    return matrices


def condense(coeffs, element_loads, basis_mats):
    element_mats = jnp.einsum("ek,kab->eab", coeffs, basis_mats, precision=full_precision)
    inner_block = element_mats[:, :CELL_DOFS, :CELL_DOFS]
    coupling = element_mats[:, :CELL_DOFS, CELL_DOFS:]
    outer_block = element_mats[:, CELL_DOFS:, CELL_DOFS:]
    factor = jnp.linalg.cholesky(inner_block)
    solved = jax.scipy.linalg.solve_triangular(factor, coupling, lower=True)
    source = jax.scipy.linalg.solve_triangular(
        factor, element_loads[:, :CELL_DOFS, None], lower=True
    )[:, :, 0]
    schur_part = outer_block - jnp.einsum("eib,eic->ebc", solved, solved, precision=full_precision)
    load_trace = element_loads[:, CELL_DOFS:] - jnp.einsum(
        "eib,ei->eb", solved, source, precision=full_precision
    )
    return (schur_part, load_trace)


def condense_blocks(coeffs, element_loads, basis_mats):
    elem_count = coeffs.shape[0]
    block_rows = math.gcd(elem_count, 16)
    grouped = (
        coeffs.reshape(-1, block_rows, coeffs.shape[1]),
        element_loads.reshape(-1, block_rows, element_loads.shape[1]),
    )
    schur_part, load_trace = lax.map(
        lambda pieces: condense(pieces[0], pieces[1], basis_mats), grouped
    )
    return (
        schur_part.reshape(elem_count, TRACE_DOFS, TRACE_DOFS),
        load_trace.reshape(elem_count, TRACE_DOFS),
    )


def pick_columns(fields, columns):
    picked = fields[:, :, columns]
    return jnp.moveaxis(picked, 2, 0).reshape(2, -1)


def place_rows(fields, columns, arrived):
    shaped = jnp.moveaxis(arrived.reshape(2, fields.shape[0], FACE_DOFS, SHARED), 0, 2)
    return fields.at[:, :, columns].add(shaped)


def owned_dot(first, second):
    return jnp.sum(first * second)


def on_device(
    basis_mats,
    coeffs,
    element_loads,
    elem_faces,
    orient_codes,
    shared_owned,
    shared_remote,
    lower_peers,
    upper_peers,
):
    elem_count = coeffs.shape[0]
    extent = FACE_DEV + REMOTE
    size_outer = lax.axis_size("gx")
    size_inner = lax.axis_size("gy")
    devices = size_outer * size_inner
    schur_blocks, load_trace = condense_blocks(coeffs, element_loads, basis_mats)
    choose = (orient_codes[:, :, None] == jnp.arange(8, dtype=jnp.int32)[None, None, :]).astype(
        jnp.float32
    )
    permute = jnp.einsum(
        "ejo,oqp->ejqp", choose, jnp.asarray(permute_mats()), precision=full_precision
    )
    incidence = (
        elem_faces.reshape(-1)[:, None] == jnp.arange(extent, dtype=jnp.int32)[None, :]
    ).astype(jnp.float32)
    owned_lists = shared_owned[0]
    remote_lists = FACE_DEV + shared_remote[0]
    lower_ids = lower_peers[0]
    upper_ids = upper_peers[0]

    def collect(element_values):
        shaped = element_values.reshape(elem_count, 6, FACE_DOFS)
        placed = jnp.einsum("ejqp,ejq->ejp", permute, shaped, precision=full_precision)
        return jnp.dot(
            placed.reshape(elem_count * 6, FACE_DOFS).T, incidence, precision=full_precision
        )

    fields = jnp.stack([collect(load_trace), collect(jnp.diagonal(schur_blocks, axis1=1, axis2=2))])

    def upward_bucket(partial_value):
        outgoing = pick_columns(partial_value, remote_lists)
        bucket = jnp.zeros((devices, outgoing.shape[1]), jnp.float32).at[upper_ids].set(outgoing)
        return bucket.reshape(size_outer, size_inner, -1)

    def upward_settle(partial_value, arrived):
        incoming = arrived.reshape(devices, -1)[lower_ids]
        return place_rows(partial_value[:, :, :FACE_DEV], owned_lists, incoming)

    def downward_bucket(values):
        outgoing = pick_columns(values[None], owned_lists)
        bucket = jnp.zeros((devices, outgoing.shape[1]), jnp.float32).at[lower_ids].set(outgoing)
        return bucket.reshape(size_outer, size_inner, -1)

    arrived = lax.all_to_all(
        lax.all_to_all(upward_bucket(fields), "gx", split_axis=0, concat_axis=0, tiled=True),
        "gy",
        split_axis=1,
        concat_axis=1,
        tiled=True,
    )
    settled = upward_settle(fields, arrived)
    rhs_faces = settled[0]
    diag_faces = settled[1]

    def rz_total(residual, precond):
        return lax.psum(owned_dot(residual, precond), ("gx", "gy"))

    trace = jnp.zeros_like(rhs_faces)
    residual = rhs_faces
    precond = residual / diag_faces
    direction = precond
    rz_now = rz_total(residual, precond)
    for iteration in range(ITERS):
        fetched = lax.all_to_all(
            lax.all_to_all(
                downward_bucket(direction), "gx", split_axis=0, concat_axis=0, tiled=True
            ),
            "gy",
            split_axis=1,
            concat_axis=1,
            tiled=True,
        )
        downward_incoming = fetched.reshape(devices, -1)[upper_ids]
        remote = place_rows(
            jnp.zeros((1, FACE_DOFS, REMOTE), jnp.float32), shared_remote[0], downward_incoming
        )
        gathered = jnp.dot(
            incidence, jnp.concatenate([direction, remote[0]], axis=1).T, precision=full_precision
        ).reshape(elem_count, 6, FACE_DOFS)
        operate_partial_value = collect(
            jnp.einsum(
                "ekl,el->ek",
                schur_blocks,
                jnp.einsum("ejqp,ejp->ejq", permute, gathered, precision=full_precision).reshape(
                    elem_count, TRACE_DOFS
                ),
                precision=full_precision,
            )
        )[None]
        returned = lax.all_to_all(
            lax.all_to_all(
                upward_bucket(operate_partial_value), "gx", split_axis=0, concat_axis=0, tiled=True
            ),
            "gy",
            split_axis=1,
            concat_axis=1,
            tiled=True,
        )
        mapped = upward_settle(operate_partial_value, returned)[0]
        step_size = rz_now / lax.psum(owned_dot(direction, mapped), ("gx", "gy"))
        trace = trace + step_size * direction
        residual = residual - step_size * mapped
        if iteration + 1 < ITERS:
            precond = residual / diag_faces
            rz_next = rz_total(residual, precond)
            direction = precond + rz_next / rz_now * direction
            rz_now = rz_next
    return (trace, residual)


def solution(mesh):
    placed = (
        P(),
        P(("gx", "gy"), None),
        P(("gx", "gy"), None),
        P(("gx", "gy"), None),
        P(("gx", "gy"), None),
        P(("gx", "gy"), None, None),
        P(("gx", "gy"), None, None),
        P(("gx", "gy"), None),
        P(("gx", "gy"), None),
    )
    return jax.shard_map(
        on_device,
        mesh=mesh,
        in_specs=placed,
        out_specs=(P(None, ("gx", "gy")), P(None, ("gx", "gy"))),
        check_vma=False,
    )
```

profile of v0, /device:TPU:1, one launch (start us, length us, event | category | flops | bytes accessed | tf_op | source)
XLA Modules:
  0.0 1485.4 jit_solution(4220468989809825634)
XLA Ops:
  1.3 9.7 fusion
  16.7 183.1 %custom-call.13 = f32[16,125,125]{2,1,0:T(8,128)S(1)} custom-call(f32[16,125,125]{2,1,0:T(8,128)S(1)} %fusion.20), custom_call_target="Cholesky" | custom-call | tf_op jit(solution)/shard_map/while/body/eval_jaxpr/jit(cholesky)/cholesky | solution.py:53
  200.3 153.7 %custom-call.14 = f32[16,1,125,125]{2,3,1,0:T(8,128)S(1)} custom-call(f32[16,1,125,125]{3,2,1,0:T(8,128)S(1)} %select_bitcast_fusion), custom_call_target="InvertDiagBlocksLowerTriangular" | custom-call | tf_op jit(solution)/shard_map/while/body/eval_jaxpr/jit(_solve_triangular)/vmap()/triangular_solve | solution.py:54
  396.4 22.3 %all_to_all.90 = f32[8,64,200]{2,1,0:T(8,128)S(1)} all-to-all(f32[8,64,200]{2,1,0:T(8,128)S(1)} %bitcast.301), channel_id=1, replica_groups=mesh['gx'=8,'gy'=64] {'gx'}, dimensions={0} | all-to-all | bytes 819200 | tf_op jit(solution)/shard_map/all_to_all | solution.py:150
  419.8 16.9 %all-to-all-start.1 = ((f32[8,64,200]{2,0,1:T(8,128)}), f32[8,64,200]{2,0,1:T(8,128)S(1)}, u32[]{:S(2)}, u32[]{:S(2)}) async-start(f32[8,64,200]{2,0,1:T(8,128)} %copy.275), calls=%async_computation.1 | async-start | bytes 1048576 | tf_op jit(solution)/shard_map/all_to_all | solution.py:149
  437.0 17.0 %all-to-all-done.1 = f32[8,64,200]{2,0,1:T(8,128)S(1)} async-done(((f32[8,64,200]{2,0,1:T(8,128)}), f32[8,64,200]{2,0,1:T(8,128)S(1)}, u32[]{:S(2)}, u32[]{:S(2)}) %all-to-all-start.1) | async-done | bytes 409632 | tf_op jit(solution)/shard_map/all_to_all | solution.py:149
  459.1 14.8 all_to_all.91
  481.1 11.8 all-to-all-done.3
  508.7 14.6 all_to_all.92
  530.4 11.9 all-to-all-done.5
  544.3 95.6 %all-reduce = (f32[]{:T(128)}, f32[]{:T(128)}) all-reduce(f32[]{:T(128)} %get-tuple-element.33, f32[]{:T(128)} %get-tuple-element.32), channel_id=1, replica_groups=mesh['gx'=8,'gy'=64] {'gx','gy'}, use_global_device_ids=true, to_apply=%region_5.6 | all-reduce | flops 2 | bytes 16 | tf_op jit(solution)/shard_map/psum | solution.py:161
  641.8 93.4 %psum.58 = f32[]{:T(128)} all-reduce(f32[]{:T(128)} %get-tuple-element.44), channel_id=1, replica_groups=mesh['gx'=8,'gy'=64] {'gx','gy'}, use_global_device_ids=true, to_apply=%region_13.14 | all-reduce | flops 1 | bytes 8 | tf_op jit(solution)/shard_map/psum | solution.py:161
  738.1 15.0 %all_to_all.93 = f32[8,64,100]{2,1,0:T(8,128)S(1)} all-to-all(f32[8,64,100]{2,1,0:T(8,128)S(1)} %bitcast.307), channel_id=1, replica_groups=mesh['gx'=8,'gy'=64] {'gx'}, dimensions={0} | all-to-all | bytes 409600 | tf_op jit(solution)/shard_map/all_to_all | solution.py:170
  753.9 8.2 all-to-all-start.7
  762.2 11.9 all-to-all-done.7
  789.5 14.6 all_to_all.94
  811.2 11.9 all-to-all-done.9
  825.1 95.5 %psum.59 = f32[]{:T(128)} all-reduce(f32[]{:T(128)} %multiply_reduce_fusion.4), channel_id=1, replica_groups=mesh['gx'=8,'gy'=64] {'gx','gy'}, use_global_device_ids=true, to_apply=%region_19.20 | all-reduce | flops 1 | bytes 8 | tf_op jit(solution)/shard_map/psum | solution.py:205
  922.6 93.9 %psum.60 = f32[]{:T(128)} all-reduce(f32[]{:T(128)} %get-tuple-element.40), channel_id=1, replica_groups=mesh['gx'=8,'gy'=64] {'gx','gy'}, use_global_device_ids=true, to_apply=%region_21.22 | all-reduce | flops 1 | bytes 8 | tf_op jit(solution)/shard_map/psum | solution.py:161
  1019.3 14.9 %all_to_all.95 = f32[8,64,100]{2,1,0:T(8,128)S(1)} all-to-all(f32[8,64,100]{2,1,0:T(8,128)S(1)} %bitcast.309), channel_id=1, replica_groups=mesh['gx'=8,'gy'=64] {'gx'}, dimensions={0} | all-to-all | bytes 409600 | tf_op jit(solution)/shard_map/all_to_all | solution.py:170
  1035.1 8.0 all-to-all-start.11
  1043.2 11.9 all-to-all-done.11
  1070.5 14.6 all_to_all.96
  1092.2 11.9 all-to-all-done.13
  1106.3 95.5 %psum.61 = f32[]{:T(128)} all-reduce(f32[]{:T(128)} %multiply_reduce_fusion.2), channel_id=1, replica_groups=mesh['gx'=8,'gy'=64] {'gx','gy'}, use_global_device_ids=true, to_apply=%region_27.28 | all-reduce | flops 1 | bytes 8 | tf_op jit(solution)/shard_map/psum | solution.py:205
  1203.8 93.5 %psum.62 = f32[]{:T(128)} all-reduce(f32[]{:T(128)} %get-tuple-element.36), channel_id=1, replica_groups=mesh['gx'=8,'gy'=64] {'gx','gy'}, use_global_device_ids=true, to_apply=%region_29.30 | all-reduce | flops 1 | bytes 8 | tf_op jit(solution)/shard_map/psum | solution.py:161
  1300.2 14.9 %all_to_all.97 = f32[8,64,100]{2,1,0:T(8,128)S(1)} all-to-all(f32[8,64,100]{2,1,0:T(8,128)S(1)} %bitcast.304), channel_id=1, replica_groups=mesh['gx'=8,'gy'=64] {'gx'}, dimensions={0} | all-to-all | bytes 409600 | tf_op jit(solution)/shard_map/all_to_all | solution.py:170
  1316.0 8.0 all-to-all-start.15
  1324.0 11.9 all-to-all-done.15
  1351.4 14.6 all_to_all.98
  1373.0 11.9 all-to-all-done.17
  1387.0 95.5 %psum.63 = f32[]{:T(128)} all-reduce(f32[]{:T(128)} %multiply_reduce_fusion), channel_id=1, replica_groups=mesh['gx'=8,'gy'=64] {'gx','gy'}, use_global_device_ids=true, to_apply=%region_35.36 | all-reduce | flops 1 | bytes 8 | tf_op jit(solution)/shard_map/psum | solution.py:205
  (251 shorter events, 171.5 us)
Async XLA Ops:
  0.6 0.7 copy-start
  11.1 2.8 copy-start.2
  354.0 5.9 slice-start
  360.9 5.6 copy-start.4
  360.9 5.9 copy-start.3
  360.9 5.9 copy-start.5
  370.6 2.7 copy-start.1
  370.6 2.6 copy-start.6
  384.0 10.7 copy-start.7
  384.0 11.7 copy-start.9
  396.4 40.5 %copy-start.8 = (s32[1,2,4]{2,1,0:T(2,128)S(1)}, s32[1,2,4]{2,1,0:T(2,128)}, u32[]{:S(2)}) copy-start(s32[1,2,4]{2,1,0:T(2,128)} %param.15) | copy-start | bytes 100
  396.4 40.6 %copy-start.10 = (s32[1,2]{1,0:T(1,128)S(1)}, s32[1,2]{1,0:T(1,128)}, u32[]{:S(2)}) copy-start(s32[1,2]{1,0:T(1,128)} %param.17) | copy-start | bytes 28
  419.8 34.2 %all-to-all-start.1 = ((f32[8,64,200]{2,0,1:T(8,128)}), f32[8,64,200]{2,0,1:T(8,128)S(1)}, u32[]{:S(2)}, u32[]{:S(2)}) async-start(f32[8,64,200]{2,0,1:T(8,128)} %copy.275), calls=%async_computation.1 | async-start | bytes 1048576 | tf_op jit(solution)/shard_map/all_to_all | solution.py:149
  474.8 18.1 %all-to-all-start.3 = ((f32[8,64,100]{2,0,1:T(8,128)}), f32[8,64,100]{2,0,1:T(8,128)S(1)}, u32[]{:S(2)}, u32[]{:S(2)}) async-start(f32[8,64,100]{2,0,1:T(8,128)} %copy.281), calls=%async_computation.3 | async-start | bytes 524288 | tf_op jit(solution)/shard_map/all_to_all | solution.py:169
  524.2 18.1 %all-to-all-start.5 = ((f32[8,64,100]{2,0,1:T(8,128)}), f32[8,64,100]{2,0,1:T(8,128)S(1)}, u32[]{:S(2)}, u32[]{:S(2)}) async-start(f32[8,64,100]{2,0,1:T(8,128)} %copy.289), calls=%async_computation.5 | async-start | bytes 524288 | tf_op jit(solution)/shard_map/all_to_all | solution.py:195
  753.9 20.1 %all-to-all-start.7 = ((f32[8,64,100]{2,0,1:T(8,128)}), f32[8,64,100]{2,0,1:T(8,128)S(1)}, u32[]{:S(2)}, u32[]{:S(2)}) async-start(f32[8,64,100]{2,0,1:T(8,128)} %copy.295), calls=%async_computation.7 | async-start | bytes 524288 | tf_op jit(solution)/shard_map/all_to_all | solution.py:169
  805.0 18.1 %all-to-all-start.9 = ((f32[8,64,100]{2,0,1:T(8,128)}), f32[8,64,100]{2,0,1:T(8,128)S(1)}, u32[]{:S(2)}, u32[]{:S(2)}) async-start(f32[8,64,100]{2,0,1:T(8,128)} %copy.303), calls=%async_computation.9 | async-start | bytes 524288 | tf_op jit(solution)/shard_map/all_to_all | solution.py:195
  1035.1 19.9 %all-to-all-start.11 = ((f32[8,64,100]{2,0,1:T(8,128)}), f32[8,64,100]{2,0,1:T(8,128)S(1)}, u32[]{:S(2)}, u32[]{:S(2)}) async-start(f32[8,64,100]{2,0,1:T(8,128)} %copy.309), calls=%async_computation.11 | async-start | bytes 524288 | tf_op jit(solution)/shard_map/all_to_all | solution.py:169
  1086.0 18.1 %all-to-all-start.13 = ((f32[8,64,100]{2,0,1:T(8,128)}), f32[8,64,100]{2,0,1:T(8,128)S(1)}, u32[]{:S(2)}, u32[]{:S(2)}) async-start(f32[8,64,100]{2,0,1:T(8,128)} %copy.317), calls=%async_computation.13 | async-start | bytes 524288 | tf_op jit(solution)/shard_map/all_to_all | solution.py:195
  1316.0 19.9 %all-to-all-start.15 = ((f32[8,64,100]{2,0,1:T(8,128)}), f32[8,64,100]{2,0,1:T(8,128)S(1)}, u32[]{:S(2)}, u32[]{:S(2)}) async-start(f32[8,64,100]{2,0,1:T(8,128)} %copy.322), calls=%async_computation.15 | async-start | bytes 524288 | tf_op jit(solution)/shard_map/all_to_all | solution.py:169
  1366.8 18.1 %all-to-all-start.17 = ((f32[8,64,100]{2,0,1:T(8,128)}), f32[8,64,100]{2,0,1:T(8,128)S(1)}, u32[]{:S(2)}, u32[]{:S(2)}) async-start(f32[8,64,100]{2,0,1:T(8,128)} %copy.330), calls=%async_computation.17 | async-start | bytes 524288 | tf_op jit(solution)/shard_map/all_to_all | solution.py:195
where the time goes:
time: 1500 us; the launch traced here: 1490 us
  blocking collectives  803 us (54%)
  other arithmetic  353 us (24%)
  waiting for transfers between devices  112 us (7%)
  matrix products  79.3 us (5%)
  starting transfers between devices  71.4 us (5%)
  local copies, waits for them, and re-layouts  55.5 us (4%)
    psum x4, blocking collectives, rz_total(): return lax.psum(owned_dot(residual, precond), ('gx', 'gy'))  376 us
    psum x3, blocking collectives, on_device(): step_size = rz_now / lax.psum(owned_dot(direction, mapped), ('gx', 'gy'))  286 us
    another operation x4, other arithmetic, condense(): factor = jnp.linalg.cholesky(inner_block)  183 us
    another operation x3, other arithmetic, condense(): solved = jax.scipy.linalg.solve_triangular(factor, coupling, lower=True)  154 us
    all_to_all x4, blocking collectives, on_device(): lax.all_to_all(downward_bucket(direction), 'gx', split_axis=0, concat_axi...  59.6 us
    all_to_all x4, blocking collectives, on_device(): lax.all_to_all(upward_bucket(operate_partial_value), 'gx', split_axis=0,...  58.5 us
    all_to_all x4, waiting for transfers between devices, on_device(): lax.all_to_all(lax.all_to_all(upward_bucket(operate_partial_value), 'gx',...  47.5 us
    all_to_all x4, waiting for transfers between devices, on_device(): lax.all_to_all(lax.all_to_all(downward_bucket(direction), 'gx', split_axi...  47.4 us
  transfers between devices with their start and end apart: 9, of which 9 were waited for; matrix products, arithmetic and copies ran while one was open for 0% of the time, Pallas kernels for 0%

commit v1 on v0

--- a/solution.py
+++ b/solution.py
@@ -202,7 +202,7 @@
             tiled=True,
         )
         mapped = upward_settle(operate_partial_value, returned)[0]
-        step_size = rz_now / lax.psum(owned_dot(direction, mapped), ("gx", "gy"))
+        step_size = rz_now / lax.psum(lax.psum(owned_dot(direction, mapped), "gy"), "gx")
         trace = trace + step_size * direction
         residual = residual - step_size * mapped
         if iteration + 1 < ITERS:

time: 1500 us -> 1770 us (1.18)
  blocking collectives: 803 us -> 1070 us
    psum x3 -> x8, blocking collectives: 286 us -> 544 us  [the longest x4 498 us: on_device(): lax.psum(owned_dot(direction, mapped), 'gy')]
where the time goes in v1:
time: 1770 us; the launch traced here: 1750 us
  blocking collectives  1070 us (60%)
  other arithmetic  353 us (20%)
  waiting for transfers between devices  112 us (6%)
  matrix products  79.3 us (4%)
  starting transfers between devices  69.4 us (4%)
  local copies, waits for them, and re-layouts  55.5 us (3%)
    psum x4, blocking collectives, on_device(): lax.psum(owned_dot(direction, mapped), 'gy')  498 us
    psum x4, blocking collectives, rz_total(): return lax.psum(owned_dot(residual, precond), ('gx', 'gy'))  390 us
    another operation x4, other arithmetic, condense(): factor = jnp.linalg.cholesky(inner_block)  183 us
    another operation x3, other arithmetic, condense(): solved = jax.scipy.linalg.solve_triangular(factor, coupling, lower=True)  154 us
    all_to_all x4, blocking collectives, on_device(): lax.all_to_all(downward_bucket(direction), 'gx', split_axis=0, concat_axi...  59.5 us
    all_to_all x4, blocking collectives, on_device(): lax.all_to_all(upward_bucket(operate_partial_value), 'gx', split_axis=0,...  58.5 us
    all_to_all x4, waiting for transfers between devices, on_device(): lax.all_to_all(lax.all_to_all(upward_bucket(operate_partial_value), 'gx',...  47.5 us
    all_to_all x4, waiting for transfers between devices, on_device(): lax.all_to_all(lax.all_to_all(downward_bucket(direction), 'gx', split_axi...  47.4 us
  transfers between devices with their start and end apart: 9, of which 9 were waited for; matrix products, arithmetic and copies ran while one was open for 0% of the time, Pallas kernels for 0%

profile of v1, /device:TPU:1, one launch (start us, length us, event | category | flops | bytes accessed | tf_op | source)
XLA Modules:
  0.0 1754.9 jit_solution(12861167341302439988)
XLA Ops:
  16.7 183.1 %custom-call.13 = f32[16,125,125]{2,1,0:T(8,128)S(1)} custom-call(f32[16,125,125]{2,1,0:T(8,128)S(1)} %fusion.20), custom_call_target="Cholesky" | custom-call | tf_op jit(solution)/shard_map/while/body/eval_jaxpr/jit(cholesky)/cholesky | solution.py:53
  200.3 153.7 %custom-call.14 = f32[16,1,125,125]{2,3,1,0:T(8,128)S(1)} custom-call(f32[16,1,125,125]{3,2,1,0:T(8,128)S(1)} %select_bitcast_fusion), custom_call_target="InvertDiagBlocksLowerTriangular" | custom-call | tf_op jit(solution)/shard_map/while/body/eval_jaxpr/jit(_solve_triangular)/vmap()/triangular_solve | solution.py:54
  396.4 22.3 %all_to_all.90 = f32[8,64,200]{2,1,0:T(8,128)S(1)} all-to-all(f32[8,64,200]{2,1,0:T(8,128)S(1)} %bitcast.301), channel_id=1, replica_groups=mesh['gx'=8,'gy'=64] {'gx'}, dimensions={0} | all-to-all | bytes 819200 | tf_op jit(solution)/shard_map/all_to_all | solution.py:150
  419.8 16.9 all-to-all-start.1
  437.0 17.0 all-to-all-done.1
  459.1 14.8 all_to_all.91
  481.1 11.8 all-to-all-done.3
  508.7 14.6 all_to_all.92
  530.4 11.9 all-to-all-done.5
  544.3 124.5 %psum.85 = f32[]{:T(128)} all-reduce(f32[]{:T(128)} %get-tuple-element.32), channel_id=1, replica_groups=mesh['gx'=8,'gy'=64] {'gy'}, use_global_device_ids=true, to_apply=%region_11.12 | all-reduce | flops 1 | bytes 8 | tf_op jit(solution)/shard_map/psum | solution.py:205
  668.8 11.6 psum.86
  680.4 98.5 %psum.84 = f32[]{:T(128)} all-reduce(f32[]{:T(128)} %get-tuple-element.33), channel_id=1, replica_groups=mesh['gx'=8,'gy'=64] {'gx','gy'}, use_global_device_ids=true, to_apply=%region_5.6 | all-reduce | flops 1 | bytes 8 | tf_op jit(solution)/shard_map/psum | solution.py:161
  780.9 94.3 %psum.87 = f32[]{:T(128)} all-reduce(f32[]{:T(128)} %get-tuple-element.42), channel_id=1, replica_groups=mesh['gx'=8,'gy'=64] {'gx','gy'}, use_global_device_ids=true, to_apply=%region_14.15 | all-reduce | flops 1 | bytes 8 | tf_op jit(solution)/shard_map/psum | solution.py:161
  878.1 15.9 all_to_all.93
  901.9 11.9 all-to-all-done.7
  929.3 14.6 all_to_all.94
  950.9 11.9 all-to-all-done.9
  964.9 124.5 %psum.88 = f32[]{:T(128)} all-reduce(f32[]{:T(128)} %multiply_reduce_fusion.4), channel_id=1, replica_groups=mesh['gx'=8,'gy'=64] {'gy'}, use_global_device_ids=true, to_apply=%region_20.21 | all-reduce | flops 1 | bytes 8 | tf_op jit(solution)/shard_map/psum | solution.py:205
  1089.4 11.6 psum.89
  1102.9 98.5 %psum.90 = f32[]{:T(128)} all-reduce(f32[]{:T(128)} %get-tuple-element.38), channel_id=1, replica_groups=mesh['gx'=8,'gy'=64] {'gx','gy'}, use_global_device_ids=true, to_apply=%region_23.24 | all-reduce | flops 1 | bytes 8 | tf_op jit(solution)/shard_map/psum | solution.py:161
  1204.3 14.5 all_to_all.95
  1227.3 11.9 all-to-all-done.11
  1254.6 14.6 all_to_all.96
  1276.3 11.9 all-to-all-done.13
  1290.3 124.5 %psum.91 = f32[]{:T(128)} all-reduce(f32[]{:T(128)} %multiply_reduce_fusion.2), channel_id=1, replica_groups=mesh['gx'=8,'gy'=64] {'gy'}, use_global_device_ids=true, to_apply=%region_29.30 | all-reduce | flops 1 | bytes 8 | tf_op jit(solution)/shard_map/psum | solution.py:205
  1414.7 11.6 psum.92
  1428.3 98.8 %psum.93 = f32[]{:T(128)} all-reduce(f32[]{:T(128)} %get-tuple-element.34), channel_id=1, replica_groups=mesh['gx'=8,'gy'=64] {'gx','gy'}, use_global_device_ids=true, to_apply=%region_32.33 | all-reduce | flops 1 | bytes 8 | tf_op jit(solution)/shard_map/psum | solution.py:161
  1529.9 14.3 all_to_all.97
  1552.7 11.9 all-to-all-done.15
  1580.0 14.6 all_to_all.98
  1601.7 11.9 all-to-all-done.17
  1615.7 124.5 %psum.94 = f32[]{:T(128)} all-reduce(f32[]{:T(128)} %multiply_reduce_fusion), channel_id=1, replica_groups=mesh['gx'=8,'gy'=64] {'gy'}, use_global_device_ids=true, to_apply=%region_38.39 | all-reduce | flops 1 | bytes 8 | tf_op jit(solution)/shard_map/psum | solution.py:205
  (256 shorter events, 214.7 us)
Async XLA Ops:
  0.6 0.7 copy-start
  11.1 2.8 copy-start.2
  354.0 5.9 slice-start
  360.9 5.6 copy-start.4
  360.9 5.9 copy-start.3
  360.9 5.9 copy-start.5
  370.6 2.7 copy-start.1
  370.6 2.6 copy-start.6
  384.0 10.7 copy-start.7
  384.0 11.7 copy-start.9
  396.4 40.5 %copy-start.8 = (s32[1,2,4]{2,1,0:T(2,128)S(1)}, s32[1,2,4]{2,1,0:T(2,128)}, u32[]{:S(2)}) copy-start(s32[1,2,4]{2,1,0:T(2,128)} %param.15) | copy-start | bytes 100
  396.4 40.6 %copy-start.10 = (s32[1,2]{1,0:T(1,128)S(1)}, s32[1,2]{1,0:T(1,128)}, u32[]{:S(2)}) copy-start(s32[1,2]{1,0:T(1,128)} %param.17) | copy-start | bytes 28
  419.8 34.2 %all-to-all-start.1 = ((f32[8,64,200]{2,0,1:T(8,128)}), f32[8,64,200]{2,0,1:T(8,128)S(1)}, u32[]{:S(2)}, u32[]{:S(2)}) async-start(f32[8,64,200]{2,0,1:T(8,128)} %copy.275), calls=%async_computation.1 | async-start | bytes 1048576 | tf_op jit(solution)/shard_map/all_to_all | solution.py:149
  474.8 18.1 %all-to-all-start.3 = ((f32[8,64,100]{2,0,1:T(8,128)}), f32[8,64,100]{2,0,1:T(8,128)S(1)}, u32[]{:S(2)}, u32[]{:S(2)}) async-start(f32[8,64,100]{2,0,1:T(8,128)} %copy.281), calls=%async_computation.3 | async-start | bytes 524288 | tf_op jit(solution)/shard_map/all_to_all | solution.py:169
  524.2 18.1 %all-to-all-start.5 = ((f32[8,64,100]{2,0,1:T(8,128)}), f32[8,64,100]{2,0,1:T(8,128)S(1)}, u32[]{:S(2)}, u32[]{:S(2)}) async-start(f32[8,64,100]{2,0,1:T(8,128)} %copy.289), calls=%async_computation.5 | async-start | bytes 524288 | tf_op jit(solution)/shard_map/all_to_all | solution.py:195
  894.8 19.0 %all-to-all-start.7 = ((f32[8,64,100]{2,0,1:T(8,128)}), f32[8,64,100]{2,0,1:T(8,128)S(1)}, u32[]{:S(2)}, u32[]{:S(2)}) async-start(f32[8,64,100]{2,0,1:T(8,128)} %copy.295), calls=%async_computation.7 | async-start | bytes 524288 | tf_op jit(solution)/shard_map/all_to_all | solution.py:169
  944.8 18.1 %all-to-all-start.9 = ((f32[8,64,100]{2,0,1:T(8,128)}), f32[8,64,100]{2,0,1:T(8,128)S(1)}, u32[]{:S(2)}, u32[]{:S(2)}) async-start(f32[8,64,100]{2,0,1:T(8,128)} %copy.303), calls=%async_computation.9 | async-start | bytes 524288 | tf_op jit(solution)/shard_map/all_to_all | solution.py:195
  1219.7 19.5 %all-to-all-start.11 = ((f32[8,64,100]{2,0,1:T(8,128)}), f32[8,64,100]{2,0,1:T(8,128)S(1)}, u32[]{:S(2)}, u32[]{:S(2)}) async-start(f32[8,64,100]{2,0,1:T(8,128)} %copy.309), calls=%async_computation.11 | async-start | bytes 524288 | tf_op jit(solution)/shard_map/all_to_all | solution.py:169
  1270.1 18.1 %all-to-all-start.13 = ((f32[8,64,100]{2,0,1:T(8,128)}), f32[8,64,100]{2,0,1:T(8,128)S(1)}, u32[]{:S(2)}, u32[]{:S(2)}) async-start(f32[8,64,100]{2,0,1:T(8,128)} %copy.317), calls=%async_computation.13 | async-start | bytes 524288 | tf_op jit(solution)/shard_map/all_to_all | solution.py:195
  1545.1 19.5 %all-to-all-start.15 = ((f32[8,64,100]{2,0,1:T(8,128)}), f32[8,64,100]{2,0,1:T(8,128)S(1)}, u32[]{:S(2)}, u32[]{:S(2)}) async-start(f32[8,64,100]{2,0,1:T(8,128)} %copy.322), calls=%async_computation.15 | async-start | bytes 524288 | tf_op jit(solution)/shard_map/all_to_all | solution.py:169
  1595.5 18.1 %all-to-all-start.17 = ((f32[8,64,100]{2,0,1:T(8,128)}), f32[8,64,100]{2,0,1:T(8,128)S(1)}, u32[]{:S(2)}, u32[]{:S(2)}) async-start(f32[8,64,100]{2,0,1:T(8,128)} %copy.330), calls=%async_computation.17 | async-start | bytes 524288 | tf_op jit(solution)/shard_map/all_to_all | solution.py:195
